TPU v7x, 128 devices: a whole 4x4x4 slice. The times are simulated.
128 devices in a mesh: prow: 8 (over x, core), pcol: 16 (over z, y).
Axes of the slice: x: 4, y: 4, z: 4, core: 2. Of those that a mesh axis runs over, the one named last changes fastest.
Arguments:
- panels: bfloat16 [2, 96, 2048, 256], P(None, 'pcol', 'prow'), may hold values from -0.59765625 to 0.59765625
- inverses: bfloat16 [2, 96, 256, 256], P(None, 'pcol', 'prow'), may hold values from -0.25 to 0.25
- dest: int32 [96, 8, 8], P('pcol', 'prow'), may hold values from 0 to 15, as said below
- target: int32 [96, 8, 8], P('pcol', 'prow'), may hold values from 0 to 1
- ancestors: float32 [2, 4096, 4096], P(None, 'prow', 'pcol'), may hold values from -6 to 6
Outputs:
- factor: bfloat16 [2, 96, 2048, 256], P(None, 'pcol', 'prow')
- schur: float32 [2, 4096, 4096], P(None, 'prow', 'pcol')
Inputs may be any that keep to these rules, and one draw needn't show every extreme that they name: `dest`: among the 48 update blocks of one device (its leaves, its block rows), at most 6 name any one process column; on every process row one process column is named by exactly 6 blocks of every device of that row.
All inputs are finite; a program needn't handle non-finite values.
Results may differ from a plain program's by a relative error of at most 0.0045.
Values may be sent and summed in bfloat16 or wider, within the bound.
A program may use at most 128 MiB of HBM per device.

v0:
```python
import jax
import jax.numpy as jnp
from jax import lax
from jax.sharding import PartitionSpec as P


def in_order(blocks, dim):
    blocks = jnp.moveaxis(blocks, 0, dim)
    lengths = blocks.shape
    return blocks.reshape(*lengths[:dim], lengths[dim] * lengths[dim + 1], *lengths[dim + 2 :])


def copy_for_each(x, axis):
    copies = jnp.broadcast_to(x, (lax.axis_size(axis), *x.shape))
    return lax.all_to_all(copies, axis, split_axis=0, concat_axis=0, tiled=True)


def gather_directly(x, axis, dim):
    return in_order(copy_for_each(x, axis), dim)


def complex_product(left_real, left_imag, right_real, right_imag, pattern):

    def single(first_operand, second):
        return jnp.einsum(pattern, first_operand, second, preferred_element_type=jnp.float32)

    real_part = single(left_real, right_real) - single(left_imag, right_imag)
    imag_part = single(left_real, right_imag) + single(left_imag, right_real)
    return jnp.stack([real_part, imag_part]).astype(jnp.bfloat16)


def local(panels, inverses, dest, target, ancestors):
    inverse_full = gather_directly(inverses, "prow", 2)
    lower_panel = complex_product(
        panels[0], panels[1], inverse_full[0], inverse_full[1], "lrk,lkc->lrc"
    )
    segment = lax.all_gather(panels, "prow", axis=2, tiled=True)
    update = complex_product(lower_panel[0], lower_panel[1], segment[0], segment[1], "lrk,lck->lrc")
    block_width = panels.shape[3]
    leaf_count = panels.shape[1]
    local_rows = panels.shape[2] // block_width
    front_blocks = update.shape[3] // block_width
    blocks = update.reshape(2, leaf_count, local_rows, block_width, front_blocks, block_width)
    blocks = blocks.transpose(1, 2, 4, 0, 3, 5).reshape(-1, 2, block_width, block_width)
    block_count = blocks.shape[0]
    column_count = lax.axis_size("pcol")
    owned_blocks = ancestors.shape[1] // block_width
    dest_flat = dest.reshape(-1)
    target_flat = target.reshape(-1)
    slot_keys = dest_flat * owned_blocks + target_flat
    select = (
        jnp.arange(column_count * owned_blocks, dtype=jnp.int32)[:, None] == slot_keys[None, :]
    ).astype(jnp.bfloat16)
    merged = jnp.dot(select, blocks.reshape(block_count, -1), preferred_element_type=jnp.float32)
    arrived = lax.all_to_all(
        merged.astype(jnp.bfloat16), "pcol", split_axis=0, concat_axis=0, tiled=True
    ).astype(merged.dtype)
    summed = jnp.sum(arrived.reshape(column_count, owned_blocks, -1), axis=0)
    summed = summed.reshape(owned_blocks, 2, block_width, block_width).transpose(1, 0, 2, 3)
    summed = summed.reshape(2, owned_blocks * block_width, block_width)
    return (lower_panel, ancestors - summed)


def solution(mesh):
    return jax.shard_map(
        local,
        mesh=mesh,
        in_specs=(
            P(None, "pcol", "prow", None),
            P(None, "pcol", "prow", None),
            P("pcol", "prow", None),
            P("pcol", "prow", None),
            P(None, "prow", "pcol"),
        ),
        out_specs=(P(None, "pcol", "prow", None), P(None, "prow", "pcol")),
        check_vma=False,
    )
```

profile of v0, /device:TPU:0, one launch (start us, length us, event | category | flops | bytes accessed | tf_op | source)
XLA Modules:
  0.0 333.0 jit_solution(2296881898128257794)
XLA Ops:
  7.2 0.0 copy-start.5
  7.2 0.0 copy-start.8
  7.2 0.0 copy-start.7
  7.2 0.0 all-gather.2.cloned.1.call-start
  7.2 0.7 all-gather.2.cloned.1.call-update
  7.9 2.3 broadcast_in_dim.2
  10.2 4.4 %all-to-all-start = ((bf16[8,2,6,32,256]{4,3,2,1,0:T(8,128)(2,1)}), bf16[8,2,6,32,256]{4,3,2,1,0:T(8,128)(2,1)S(1)}, u32[]{:S(2)}, u32[]{:S(2)}) async-start(bf16[8,2,6,32,256]{4,3,2,1,0:T(8,128)(2,1)} %broadcast_in_dim.2), calls=%async_computation | async-start | bytes 3145728 | tf_op jit(solution)/shard_map/all_to_all | solution.py:15
  14.6 0.0 copy-done.8
  14.6 0.0 copy-done.7
  14.6 0.1 add.18
  14.7 30.9 %all-to-all-done = bf16[8,2,6,32,256]{4,3,2,1,0:T(8,128)(2,1)S(1)} async-done(((bf16[8,2,6,32,256]{4,3,2,1,0:T(8,128)(2,1)}), bf16[8,2,6,32,256]{4,3,2,1,0:T(8,128)(2,1)S(1)}, u32[]{:S(2)}, u32[]{:S(2)}) %all-to-all-start) | async-done | bytes 1572896 | tf_op jit(solution)/shard_map/all_to_all | solution.py:15
  45.6 0.2 fusion.15
  45.8 0.1 copy.12
  45.9 0.1 copy.13
  45.9 0.0 copy-done.5
  45.9 0.4 fusion.8
  46.3 0.4 fusion.6
  46.7 0.4 subtract_convert_fusion.1
  47.1 0.0 copy-start
  47.1 0.4 add_convert_fusion.1
  47.5 0.0 copy-start.3
  47.5 40.9 %all-gather.2.cloned.1.call-done = bf16[2,6,2048,256]{3,2,1,0:T(8,128)(2,1)} async-done(((bf16[2,6,256,256]{3,2,1,0:T(8,128)(2,1)}), bf16[2,6,2048,256]{3,2,1,0:T(8,128)(2,1)}) %all-gather.2.cloned.1.call-update) | async-done | bytes 12582928 | tf_op jit(solution)/shard_map/all_gather | solution.py:37
  88.4 9.1 %fusion.1 = f32[6,256,2048]{2,1,0:T(8,128)} fusion(bf16[6,256,256]{2,1,0:T(8,128)(2,1)S(1)} %subtract_convert_fusion.1, bf16[2,6,2048,256]{3,2,1,0:T(8,128)(2,1)} %all-gather.2.cloned.1.call-done), kind=kOutput, calls=%fused_computation.8 | convolution fusion | flops 1610612736 | bytes 19660800 | tf_op jit(solution)/shard_map/lrk,lck->lrc/dot_general | solution.py:25
  97.5 10.9 %subtract_convert_fusion = bf16[6,256,2048]{2,1,0:T(8,128)(2,1)} fusion(f32[6,256,2048]{2,1,0:T(8,128)} %fusion.1, bf16[6,256,256]{2,1,0:T(8,128)(2,1)S(1)} %add_convert_fusion.1, bf16[2,6,2048,256]{3,2,1,0:T(8,128)(2,1)} %all-gather.2.cloned.1.call-done), kind=kOutput, calls=%fused_computation.4 | convolution fusion | flops 1616904192 | bytes 25952256 | tf_op jit(solution)/shard_map/lrk,lck->lrc/dot_general | solution.py:25
  108.5 5.7 %copy.17 = bf16[192,8,8,256]{3,2,1,0:T(8,128)(2,1)S(1)} copy(bf16[192,8,8,256]{3,1,2,0:T(8,128)(2,1)} %bitcast.66) | data formatting | bytes 12582912
  114.2 0.0 slice-start.2
  114.2 4.2 %copy.14 = bf16[1,6,1,256,8,256]{5,3,0,4,1,2:T(8,128)(2,1)} copy(bf16[1,6,1,256,8,256]{5,4,3,1,2,0:T(8,128)(2,1)S(1)} %bitcast.61) | data formatting | bytes 12582912 | tf_op jit(solution)/shard_map/stack | solution.py:29
  118.5 0.0 slice-done
  118.5 0.0 copy-start.1
  118.5 7.5 %fusion = f32[6,256,2048]{2,1,0:T(8,128)} fusion(bf16[6,256,256]{2,1,0:T(8,128)(2,1)} %copy-done.3, bf16[2,6,2048,256]{3,2,1,0:T(8,128)(2,1)S(1)} %bitcast.60), kind=kOutput, calls=%fused_computation.7 | convolution fusion | flops 1610612736 | bytes 19660800 | tf_op jit(solution)/shard_map/lrk,lck->lrc/dot_general | solution.py:25
  126.0 0.0 copy-done.1
  126.0 11.2 %add_convert_fusion = bf16[6,256,2048]{2,1,0:T(8,128)(2,1)} fusion(f32[6,256,2048]{2,1,0:T(8,128)} %fusion, bf16[6,256,256]{2,1,0:T(8,128)(2,1)S(1)} %copy-done.1, bf16[2,6,2048,256]{3,2,1,0:T(8,128)(2,1)} %all-gather.2.cloned.1.call-done), kind=kOutput, calls=%fused_computation.3 | convolution fusion | flops 1616904192 | bytes 25952256 | tf_op jit(solution)/shard_map/lrk,lck->lrc/dot_general | solution.py:25
  137.3 5.7 %copy.18 = bf16[192,8,8,256]{3,2,1,0:T(8,128)(2,1)S(1)} copy(bf16[192,8,8,256]{3,1,2,0:T(8,128)(2,1)} %bitcast.65) | data formatting | bytes 12582912
  143.0 0.0 slice-start.4
  143.0 1.5 copy.15
  144.5 0.0 slice-done.3
  144.5 0.1 slice-done.4
  144.6 5.2 %maximum_bitcast_fusion = bf16[6,1,8,2,256,256]{5,4,3,2,0,1:T(8,128)(2,1)} fusion(bf16[1,6,1,256,8,256]{5,3,0,4,1,2:T(8,128)(2,1)S(1)} %copy.15, bf16[1,6,1,256,8,256]{5,3,0,4,1,2:T(8,128)(2,1)S(1)} %bitcast.64), kind=kLoop, calls=%fused_computation.2 | loop fusion | flops 6291456 | bytes 25165824 | tf_op jit(solution)/shard_map/transpose | solution.py:44
  149.8 12.9 %reshape_reshape.3 = bf16[48,131072]{1,0:T(8,128)(2,1)} reshape(bf16[6,1,8,2,256,256]{5,4,3,2,0,1:T(8,128)(2,1)} %maximum_bitcast_fusion) | data formatting | bytes 25165824 | tf_op jit(solution)/shard_map/reshape;reshape | solution.py:54
  162.8 10.1 %convolution_convert_fusion = bf16[32,131072]{1,0:T(8,128)(2,1)} fusion(bf16[48,131072]{1,0:T(8,128)(2,1)} %reshape_reshape.3, s32[48]{0:T(128)S(1)} %add.18), kind=kOutput, calls=%fused_computation | convolution fusion | flops 406849024 | bytes 20971712 | tf_op jit(solution)/shard_map/dot_general | solution.py:54
  172.8 9.4 %all_to_all.10 = bf16[16,2,131072]{2,1,0:T(2,128)(2,1)} reshape(bf16[32,131072]{1,0:T(8,128)(2,1)} %convolution_convert_fusion) | data formatting | bytes 16777216 | tf_op jit(solution)/shard_map/all_to_all | solution.py:55
  182.2 8.2 %all-to-all-start.1 = ((bf16[16,2,131072]{2,1,0:T(2,128)(2,1)}), bf16[16,2,131072]{2,1,0:T(2,128)(2,1)}, u32[]{:S(2)}, u32[]{:S(2)}) async-start(bf16[16,2,131072]{2,1,0:T(2,128)(2,1)} %all_to_all.10), calls=%async_computation.1 | async-start | bytes 16777216 | tf_op jit(solution)/shard_map/all_to_all | solution.py:55
  190.5 1.3 pad_maximum_fusion
  191.8 124.5 %all-to-all-done.1 = bf16[16,2,131072]{2,1,0:T(2,128)(2,1)} async-done(((bf16[16,2,131072]{2,1,0:T(2,128)(2,1)}), bf16[16,2,131072]{2,1,0:T(2,128)(2,1)}, u32[]{:S(2)}, u32[]{:S(2)}) %all-to-all-start.1) | async-done | bytes 8388640 | tf_op jit(solution)/shard_map/all_to_all | solution.py:55
  316.2 8.7 %convert_reduce_fusion = f32[2,131072]{1,0:T(2,128)S(1)} fusion(bf16[16,2,131072]{2,1,0:T(2,128)(2,1)} %all-to-all-done.1), kind=kLoop, calls=%fused_computation.1 | loop fusion | flops 8126464 | bytes 9437184 | tf_op jit(solution)/shard_map/reduce_sum | solution.py:58
  324.9 0.1 copy.19
  325.0 0.1 copy.16
  325.1 1.1 bitcast_subtract_fusion
  (16 shorter events, 0.0 us)
Async XLA Ops:
  7.2 38.8 %copy-start.5 = (bf16[2,6,256,256]{3,2,1,0:T(8,128)(2,1)S(1)}, bf16[2,6,256,256]{3,2,1,0:T(8,128)(2,1)}, u32[]{:S(2)}) copy-start(bf16[2,6,256,256]{3,2,1,0:T(8,128)(2,1)} %param.5) | copy-start | bytes 4718596
  7.2 7.4 %copy-start.8 = (s32[6,1,8]{2,1,0:T(1,128)S(1)}, s32[6,1,8]{2,1,0:T(1,128)}, u32[]{:S(2)}) copy-start(s32[6,1,8]{2,1,0:T(1,128)} %param.7) | copy-start | bytes 580
  7.2 7.4 %copy-start.7 = (s32[6,1,8]{2,1,0:T(1,128)S(1)}, s32[6,1,8]{2,1,0:T(1,128)}, u32[]{:S(2)}) copy-start(s32[6,1,8]{2,1,0:T(1,128)} %param.8) | copy-start | bytes 580
  7.2 81.2 %all-gather.2.cloned.1.call-start = ((), (), s32[]{:S(2)}) async-start(), calls=%async_computation.2 | async-start | bytes 14155776 | tf_op jit(solution)/shard_map/all_gather | solution.py:37
  10.2 35.5 %all-to-all-start = ((bf16[8,2,6,32,256]{4,3,2,1,0:T(8,128)(2,1)}), bf16[8,2,6,32,256]{4,3,2,1,0:T(8,128)(2,1)S(1)}, u32[]{:S(2)}, u32[]{:S(2)}) async-start(bf16[8,2,6,32,256]{4,3,2,1,0:T(8,128)(2,1)} %broadcast_in_dim.2), calls=%async_computation | async-start | bytes 3145728 | tf_op jit(solution)/shard_map/all_to_all | solution.py:15
  47.1 50.4 %copy-start = (bf16[6,256,256]{2,1,0:T(8,128)(2,1)}, bf16[6,256,256]{2,1,0:T(8,128)(2,1)S(1)}, u32[]{:S(2)}) copy-start(bf16[6,256,256]{2,1,0:T(8,128)(2,1)S(1)} %subtract_convert_fusion.1) | copy-start | bytes 2359300
  47.5 50.0 %copy-start.3 = (bf16[6,256,256]{2,1,0:T(8,128)(2,1)}, bf16[6,256,256]{2,1,0:T(8,128)(2,1)S(1)}, u32[]{:S(2)}) copy-start(bf16[6,256,256]{2,1,0:T(8,128)(2,1)S(1)} %add_convert_fusion.1) | copy-start | bytes 2359300
  108.5 10.0 %slice-start = ((s8[12582912]{0:T(1024)(128)(4,1)}), s8[4194304]{0:T(1024)(128)(4,1)S(1)}, s32[]{:S(2)}) async-start(s8[12582912]{0:T(1024)(128)(4,1)} %bitcast.59), calls=%async_computation.3 | async-start | bytes 8388608
  108.5 10.0 %slice-start.1 = ((s8[12582912]{0:T(1024)(128)(4,1)}), s8[4194304]{0:T(1024)(128)(4,1)S(1)}, s32[]{:S(2)}) async-start(s8[12582912]{0:T(1024)(128)(4,1)} %bitcast.59), calls=%async_computation.4 | async-start | bytes 8388608
  114.2 4.3 %slice-start.2 = ((s8[12582912]{0:T(1024)(128)(4,1)}), s8[4194304]{0:T(1024)(128)(4,1)S(1)}, s32[]{:S(2)}) async-start(s8[12582912]{0:T(1024)(128)(4,1)} %bitcast.59), calls=%async_computation.5 | async-start | bytes 8388608
  118.5 7.6 %copy-start.1 = (bf16[6,256,256]{2,1,0:T(8,128)(2,1)S(1)}, bf16[6,256,256]{2,1,0:T(8,128)(2,1)}, u32[]{:S(2)}) copy-start(bf16[6,256,256]{2,1,0:T(8,128)(2,1)} %copy-done) | copy-start | bytes 2359300
  137.3 7.2 %slice-start.3 = ((s8[6291456]{0:T(1024)(128)(4,1)}), s8[4194304]{0:T(1024)(128)(4,1)S(1)}, s32[]{:S(2)}) async-start(s8[6291456]{0:T(1024)(128)(4,1)} %bitcast.63), calls=%async_computation.6 | async-start | bytes 8388608
  143.0 1.6 slice-start.4
  182.2 8.2 %copy-start.2 = (bf16[6,256,256]{2,1,0:T(8,128)(2,1)S(1)}, bf16[6,256,256]{2,1,0:T(8,128)(2,1)}, u32[]{:S(2)}) copy-start(bf16[6,256,256]{2,1,0:T(8,128)(2,1)} %copy-done) | copy-start | bytes 2359300
  182.2 8.3 %copy-start.4 = (bf16[6,256,256]{2,1,0:T(8,128)(2,1)S(1)}, bf16[6,256,256]{2,1,0:T(8,128)(2,1)}, u32[]{:S(2)}) copy-start(bf16[6,256,256]{2,1,0:T(8,128)(2,1)} %copy-done.3) | copy-start | bytes 2359300
  182.2 134.0 %all-to-all-start.1 = ((bf16[16,2,131072]{2,1,0:T(2,128)(2,1)}), bf16[16,2,131072]{2,1,0:T(2,128)(2,1)}, u32[]{:S(2)}, u32[]{:S(2)}) async-start(bf16[16,2,131072]{2,1,0:T(2,128)(2,1)} %all_to_all.10), calls=%async_computation.1 | async-start | bytes 16777216 | tf_op jit(solution)/shard_map/all_to_all | solution.py:55
  191.8 133.3 %copy-start.6 = (f32[2,512,256]{2,1,0:T(8,128)S(1)}, f32[2,512,256]{2,1,0:T(8,128)}, u32[]{:S(2)}) copy-start(f32[2,512,256]{2,1,0:T(8,128)} %param.9) | copy-start | bytes 3145732
Sparse Core Ops, SparseCore 0:
  9.7 78.6 all-gather.1
where the time goes:
time: 334 us; the launch traced here: 333 us
  waiting for transfers between devices  197 us (59%)
  matrix products  50.4 us (15%)
  local copies, waits for them, and re-layouts  42.4 us (13%)
  other arithmetic  16.3 us (5%)
  between operations  14.3 us (4%)
  starting transfers between devices  12.7 us (4%)
    all_to_all x1, waiting for transfers between devices, local(): lax.all_to_all(merged.astype(jnp.bfloat16), 'pcol', split_axis=0, concat_...  124 us
    all_gather x1, waiting for transfers between devices, local(): segment = lax.all_gather(panels, 'prow', axis=2, tiled=True)  40.9 us
    dot_general x8, matrix products, single(): jnp.einsum(pattern, first_operand, second, preferred_element_type=jnp.flo...  40.3 us
    all_to_all x1, waiting for transfers between devices, copy_for_each(): return lax.all_to_all(copies, axis, split_axis=0, concat_axis=0, tiled=True)  30.9 us
    another operation x1, local copies, waits for them, and re-layouts, local(): blocks.reshape(block_count, -1)  12.9 us
    unnamed x31, local copies, waits for them, and re-layouts  11.7 us
    dot_general x1, matrix products, local(): jnp.dot(select, blocks.reshape(block_count, -1), preferred_element_type=j...  10.1 us
    all_to_all x1, local copies, waits for them, and re-layouts, local(): lax.all_to_all(merged.astype(jnp.bfloat16), 'pcol', split_axis=0, concat_...  9.39 us
  transfers between devices with their start and end apart: 3, of which 3 were waited for; matrix products, arithmetic and copies ran while one was open for 2% of the time, Pallas kernels for 0%

commit v1 on v0

v1 whole, which is shorter than its diff:
```python
import functools

import jax
import jax.numpy as jnp
from jax import lax
from jax.experimental import pallas as pl
from jax.experimental.pallas import tpu as pltpu
from jax.sharding import PartitionSpec as P

MESH = pl.DeviceIdType.MESH
CHUNKS = 8
RING = 4
CAP = 6


def dot(a, b):
    return jnp.dot(a, b, preferred_element_type=jnp.float32)


def dot_t(a, b):
    return lax.dot_general(a, b, (((1,), (1,)), ((), ())), preferred_element_type=jnp.float32)


def kernel(
    table, panels, inverses, factor, summed,
    pan, inv, fac, upd, mer, t1, g1, t2, g2, res,
    psend, precv, isend, irecv, rsend, rrecv, load, store,
):
    n_chunks, _, leaves, rows_b, h, width = pan.shape
    part = inverses.shape[2]
    px, pc = lax.axis_index("prow"), lax.axis_index("pcol")
    x, core = px // 2, px % 2
    z, y = pc // RING, pc % RING

    def at_x(step, other=0):
        return ((x + step) % RING) * 2 + (core if not other else 1 - core)

    def at_yz(dy, dz):
        return ((z + dz) % RING) * RING + (y + dy) % RING

    x_next, x_prev, mate = (at_x(1), pc), (at_x(3), pc), (at_x(0, 1), pc)
    y_next, y_prev = (px, at_yz(1, 0)), (px, at_yz(3, 0))
    z_next, z_prev = (px, at_yz(0, 1)), (px, at_yz(0, 3))

    def remote(src, dst, send, recv, device):
        return pltpu.make_async_remote_copy(
            src_ref=src, dst_ref=dst, send_sem=send, recv_sem=recv,
            device_id=device, device_id_type=MESH,
        )

    def gather_copy(view, send, recv, n):
        blocks = (px, px, px, at_x(3), at_x(1), at_x(3), at_x(1), at_x(2), at_x(2))
        planes = (None, None, None, 0, 1, None, None, 0, 1)
        devices = (x_next, x_prev, mate, x_next, x_prev, mate, mate, mate, mate)
        src = view(blocks[n], planes[n])
        return remote(src, src, send(n), recv(n), devices[n])

    def gather_wait(view, send, recv, n):
        blocks = (
            at_x(3), at_x(1), at_x(0, 1), at_x(2), at_x(2),
            at_x(3, 1), at_x(1, 1), at_x(2, 1), at_x(2, 1),
        )
        planes = (None, None, None, 0, 1, None, None, 0, 1)
        dst = view(blocks[n], planes[n])
        remote(dst, dst, send(n), recv(n), mate).wait_recv()

    def pan_args(k):
        def view(block, plane):
            return pan.at[k, :, :, block] if plane is None else pan.at[k, plane, :, block]

        return view, (lambda n: psend.at[k, n]), (lambda n: precv.at[k, n])

    def inv_view(block, plane):
        rows = pl.ds(pl.multiple_of(block * part, part), part)
        return inv.at[:, :, rows] if plane is None else inv.at[plane, :, rows]

    inv_args = (inv_view, (lambda n: isend.at[n]), (lambda n: irecv.at[n]))

    def sum_copy(k, half, n):
        first_next, first_prev = (y_next, y_prev) if half == 0 else (z_next, z_prev)
        then_next, then_prev = (z_next, z_prev) if half == 0 else (y_next, y_prev)
        m, t, g = mer.at[k, half], t1.at[k, half], g1.at[k, half]
        tt, gg = t2.at[k, half], g2.at[k, half]
        src, dst, device = (
            (m.at[2, 0:2], t.at[0], first_next),
            (m.at[2, 2:4], t.at[1], first_prev),
            (m.at[1, 2:4], g.at[0, 2:4], first_next),
            (m.at[3, 0:2], g.at[1, 0:2], first_prev),
            (m.at[1, 0:2], g.at[0, 0:2], first_next),
            (m.at[3, 2:4], g.at[1, 2:4], first_prev),
            (m.at[0, 2, 0], tt.at[0], then_next),
            (m.at[0, 2, 1], tt.at[1], then_prev),
            (m.at[0, 1, 1], gg.at[0, 1], then_next),
            (m.at[0, 3, 0], gg.at[1, 0], then_prev),
            (m.at[0, 1, 0], gg.at[0, 0], then_next),
            (m.at[0, 3, 1], gg.at[1, 1], then_prev),
        )[n]
        return remote(src, dst, rsend.at[k, half * 12 + n], rrecv.at[k, half * 12 + n], device)

    def load_pan(k):
        rows = pl.ds(pl.multiple_of(k * h, h), h)
        return pltpu.make_async_copy(panels.at[:, :, rows], pan.at[k, :, :, px], load.at[k])

    load_inv = pltpu.make_async_copy(inverses, inv_view(px, None), load.at[n_chunks])
    store_factor = pltpu.make_async_copy(fac.at[0:2], factor, store.at[n_chunks])

    def store_sum(k):
        rows = pl.ds(pl.multiple_of(k * h, h), h)
        return pltpu.make_async_copy(res.at[k], summed.at[:, :, rows], store.at[k])

    load_inv.start()
    for k in range(n_chunks):
        load_pan(k).start()

    barrier = pltpu.get_barrier_semaphore()
    neighbours = (x_next, x_prev, mate, y_next, y_prev, z_next, z_prev)
    for device in neighbours:
        pl.semaphore_signal(barrier, inc=1, device_id=device, device_id_type=MESH)
    upd[upd.shape[0] - 1] = jnp.zeros(upd.shape[1:], upd.dtype)
    pl.semaphore_wait(barrier, len(neighbours))

    load_inv.wait()
    for n in (0, 1, 2):
        gather_copy(*inv_args, n).start()
    for k in range(n_chunks):
        load_pan(k).wait()
    for n in (0, 1, 2):
        gather_copy(*pan_args(0), n).start()
    for n in (0, 1):
        gather_wait(*inv_args, n)
    for n in (3, 4, 5, 6):
        gather_copy(*inv_args, n).start()
    for n in (0, 1, 2):
        gather_copy(*pan_args(1), n).start()

    def in_turn(k, stage):
        @pl.when(jnp.logical_and(k >= 0, k < n_chunks))
        def _():
            stage(k)

    def relay_first(k):
        for n in (0, 1):
            gather_wait(*pan_args(k), n)
        for n in (3, 4, 5, 6):
            gather_copy(*pan_args(k), n).start()

        @pl.when(k + 2 < n_chunks)
        def _():
            for n in (0, 1, 2):
                gather_copy(*pan_args(k + 2), n).start()

    def relay_second(k):
        for n in (3, 4):
            gather_wait(*pan_args(k), n)
        for n in (7, 8):
            gather_copy(*pan_args(k), n).start()

    def make_factor():
        for n in (3, 4):
            gather_wait(*inv_args, n)
        for n in (7, 8):
            gather_copy(*inv_args, n).start()
        for n in (2, 5, 6, 7, 8):
            gather_wait(*inv_args, n)

        def leaf(s, carry):
            real = pan[:, 0, s, px].reshape(width, width)
            imag = pan[:, 1, s, px].reshape(width, width)
            inv_real, inv_imag = inv[0, s], inv[1, s]
            fac[0, s] = (dot(real, inv_real) - dot(imag, inv_imag)).astype(fac.dtype)
            turned = dot(real, inv_imag) + dot(imag, inv_real)
            fac[1, s] = turned.astype(fac.dtype)
            fac[2, s] = (-turned).astype(fac.dtype)
            return carry

        lax.fori_loop(0, leaves, leaf, 0)
        store_factor.start()

    def multiply(k):
        for n in (2, 5, 6, 7, 8):
            gather_wait(*pan_args(k), n)

        def leaf(s, carry):
            real = pan[k, 0, s].reshape(rows_b * h, width)
            imag = pan[k, 1, s].reshape(rows_b * h, width)
            first = pl.multiple_of(s * rows_b, rows_b)
            product = dot_t(real, fac[0, s]) + dot_t(imag, fac[2, s])
            upd[pl.ds(first, rows_b), 0] = product.astype(upd.dtype).reshape(rows_b, h, width)
            product = dot_t(real, fac[1, s]) + dot_t(imag, fac[0, s])
            upd[pl.ds(first, rows_b), 1] = product.astype(upd.dtype).reshape(rows_b, h, width)
            return carry

        lax.fori_loop(0, leaves, leaf, 0)

        def merge(q, carry):
            half, f, g = q // 16, (q // 4) % 4, q % 4
            owner = at_yz(f + half * (g - f), g + half * (f - g))
            entry = (owner * 2 + half) * CAP
            total = upd[table[entry]].astype(jnp.float32)
            for i in range(1, CAP):
                total += upd[table[entry + i]].astype(jnp.float32)
            mer[k, half, f, g] = total.astype(mer.dtype)
            return carry

        lax.fori_loop(0, 32, merge, 0)
        for n in (0, 1, 2, 3):
            for half in (0, 1):
                sum_copy(k, half, n).start()

    def add_to(ref, other):
        ref[...] = (ref[...].astype(jnp.float32) + other[...].astype(jnp.float32)).astype(ref.dtype)

    def sum_b(k):
        for half in (0, 1):
            for n in (0, 1):
                sum_copy(k, half, n).wait_recv()
            add_to(mer.at[k, half, 1, 0:2], t1.at[k, half, 0])
            add_to(mer.at[k, half, 3, 2:4], t1.at[k, half, 1])
        for half in (0, 1):
            for n in (4, 5):
                sum_copy(k, half, n).start()

    def sum_c(k):
        for half in (0, 1):
            for n in (2, 3, 4, 5):
                sum_copy(k, half, n).wait_recv()
            total = mer[k, half, 0].astype(jnp.float32)
            total += g1[k, half, 0].astype(jnp.float32)
            total += g1[k, half, 1].astype(jnp.float32)
            mer[k, half, 0] = total.astype(mer.dtype)
        for n in (6, 7, 8, 9):
            for half in (0, 1):
                sum_copy(k, half, n).start()

    def sum_d(k):
        for half in (0, 1):
            for n in (6, 7):
                sum_copy(k, half, n).wait_recv()
            add_to(mer.at[k, half, 0, 1, 0], t2.at[k, half, 0])
            add_to(mer.at[k, half, 0, 3, 1], t2.at[k, half, 1])
        for half in (0, 1):
            for n in (10, 11):
                sum_copy(k, half, n).start()

    def sum_e(k):
        for half in (0, 1):
            for n in (8, 9, 10, 11):
                sum_copy(k, half, n).wait_recv()
            total = mer[k, half, 0, 0].astype(jnp.float32)
            total += g2[k, half, 0].astype(jnp.float32)
            total += g2[k, half, 1].astype(jnp.float32)
            res[k, half] = total
        store_sum(k).start()

    def step(i, carry):
        in_turn(i, relay_first)
        in_turn(i - 1, relay_second)
        pl.when(i == 1)(make_factor)
        in_turn(i - 6, sum_e)
        in_turn(i - 5, sum_d)
        in_turn(i - 4, sum_c)
        in_turn(i - 3, sum_b)
        in_turn(i - 2, multiply)
        return carry

    lax.fori_loop(0, n_chunks + 7, step, 0)

    for n in range(9):
        gather_copy(*inv_args, n).wait_send()

    def drain(k, carry):
        for n in range(9):
            gather_copy(*pan_args(k), n).wait_send()
        for half in (0, 1):
            for n in range(12):
                sum_copy(k, half, n).wait_send()
        store_sum(k).wait()
        return carry

    lax.fori_loop(0, n_chunks, drain, 0)
    store_factor.wait()


def local(panels, inverses, dest, target, ancestors):
    _, leaves, rows, width = panels.shape
    rows_b = dest.shape[2]
    h = rows // CHUNKS
    blocks = leaves * rows_b
    slots = RING * RING * 2
    keys = (dest * 2 + target).reshape(-1)
    order = jnp.arange(blocks, dtype=jnp.int32)
    same = (keys[:, None] == keys[None, :]) & (order[None, :] < order[:, None])
    rank = jnp.sum(same.astype(jnp.int32), axis=1)
    place = keys * CAP + rank
    hit = jnp.arange(slots * CAP, dtype=jnp.int32)[:, None] == place[None, :]
    table = jnp.min(jnp.where(hit, order[None, :], blocks), axis=1).astype(jnp.int32)

    bf16, f32 = jnp.bfloat16, jnp.float32
    any_space = pl.BlockSpec(memory_space=pl.ANY)
    dma = pltpu.SemaphoreType.DMA
    factor, summed = pl.pallas_call(
        kernel,
        out_shape=(
            jax.ShapeDtypeStruct(panels.shape, bf16),
            jax.ShapeDtypeStruct((2, 2, rows, width), f32),
        ),
        in_specs=[pl.BlockSpec(memory_space=pltpu.SMEM), any_space, any_space],
        out_specs=(any_space, any_space),
        scratch_shapes=[
            pltpu.VMEM((CHUNKS, 2, leaves, rows_b, h, width), bf16),
            pltpu.VMEM((2, leaves, width, width), bf16),
            pltpu.VMEM((3, leaves, rows, width), bf16),
            pltpu.VMEM((blocks + 1, 2, h, width), bf16),
            pltpu.VMEM((CHUNKS, 2, 4, 4, 2, h, width), bf16),
            pltpu.VMEM((CHUNKS, 2, 2, 2, 2, h, width), bf16),
            pltpu.VMEM((CHUNKS, 2, 2, 4, 2, h, width), bf16),
            pltpu.VMEM((CHUNKS, 2, 2, h, width), bf16),
            pltpu.VMEM((CHUNKS, 2, 2, 2, h, width), bf16),
            pltpu.VMEM((CHUNKS, 2, 2, h, width), f32),
            dma((CHUNKS, 9)), dma((CHUNKS, 9)), dma((9,)), dma((9,)),
            dma((CHUNKS, 24)), dma((CHUNKS, 24)), dma((CHUNKS + 1,)), dma((CHUNKS + 1,)),
        ],
        compiler_params=pltpu.CompilerParams(
            collective_id=0, has_side_effects=True, vmem_limit_bytes=60 * 1024 * 1024
        ),
    )(table, panels, inverses)
    summed = summed.transpose(1, 0, 3, 2).reshape(ancestors.shape)
    return factor, ancestors - summed


def solution(mesh):
    return jax.shard_map(
        local,
        mesh=mesh,
        in_specs=(
            P(None, "pcol", "prow", None),
            P(None, "pcol", "prow", None),
            P("pcol", "prow", None),
            P("pcol", "prow", None),
            P(None, "prow", "pcol"),
        ),
        out_specs=(P(None, "pcol", "prow", None), P(None, "prow", "pcol")),
        check_vma=False,
    )
```

time: 334 us -> 120 us (0.36)
  waiting for transfers between devices: 197 us -> 0 us
  Pallas kernels: 0 us -> 113 us
  matrix products: 50.4 us -> 0 us
  local copies, waits for them, and re-layouts: 42.4 us -> 3.45 us
  other arithmetic: 16.3 us -> 2.67 us
  between operations: 14.3 us -> 0.67 us
  starting transfers between devices: 12.7 us -> 0 us
    all_to_all x2 -> x0, waiting for transfers between devices: 155 us -> none  [the longest x1 124 us: local(): lax.all_to_all(merged.astype(jnp.bfloat16), 'pcol', split_axis=0, concat_...]
    pallas_call x0 -> x1, Pallas kernels: none -> 113 us  [local(): pl.pallas_call(kernel, out_shape=(jax.ShapeDtypeStruct(panels.shape, bf16...]
    dot_general x9 -> x0, matrix products: 50.4 us -> none  [the longest x8 40.3 us: single(): jnp.einsum(pattern, first_operand, second, preferred_element_type=jnp.flo...]
    all_gather x1 -> x0, waiting for transfers between devices: 40.9 us -> none  [local(): segment = lax.all_gather(panels, 'prow', axis=2, tiled=True)]
    another operation x3 -> x0, local copies, waits for them, and re-layouts: 18.6 us -> none  [the longest x1 12.9 us: local(): blocks.reshape(block_count, -1)]
    all_to_all x2 -> x0, starting transfers between devices: 12.6 us -> none  [the longest x1 8.23 us: local(): lax.all_to_all(merged.astype(jnp.bfloat16), 'pcol', split_axis=0, concat_...]
    unnamed x31 -> x5, local copies, waits for them, and re-layouts: 11.7 us -> 1.82 us
    all_to_all x1 -> x0, local copies, waits for them, and re-layouts: 9.39 us -> none  [local(): lax.all_to_all(merged.astype(jnp.bfloat16), 'pcol', split_axis=0, concat_...]
  transfers between devices with their start and end apart: 3 -> 0, of which waited for: 3 -> 0; matrix products, arithmetic and copies ran while one was open for 2% -> 0% of each run, Pallas kernels for 0% -> 0%
where the time goes in v1:
time: 120 us
  Pallas kernels  113 us (94%)
  local copies, waits for them, and re-layouts  3.45 us (3%)
  other arithmetic  2.67 us (2%)
    pallas_call x1, Pallas kernels, local(): pl.pallas_call(kernel, out_shape=(jax.ShapeDtypeStruct(panels.shape, bf16...  113 us

profile of v1, /device:TPU:0, one launch (start us, length us, event | category | flops | bytes accessed | tf_op | source)
XLA Modules:
  0.0 119.7 jit_solution(7189139465457775202)
XLA Ops:
  0.6 0.7 add_reduce_fusion
  1.4 0.1 reshape.20
  1.4 0.2 convert_reduce_fusion
  1.6 0.7 select_reduce_fusion.table
  2.3 0.0 copy-start.1
  2.3 112.9 %shard_map.68 = (bf16[2,6,256,256]{3,2,1,0:T(8,128)(2,1)}, f32[2,2,256,256]{3,2,1,0:T(8,128)}) custom-call(s32[192]{0:T(256)} %select_reduce_fusion.table, bf16[2,6,256,256]{3,2,1,0:T(8,128)(2,1)} %panels.1, bf16[2,6,32,256]{3,2,1,0:T(8,128)(2,1)} %inverses.1), custom_call_target="tpu_custom_call" | custom-call | tf_op jit(solution)/shard_map/pallas_call | solution.py:301
  115.2 1.6 %copy.8 = f32[2,2,256,256]{3,2,1,0:T(8,128)S(1)} copy(f32[2,2,256,256]{2,3,0,1:T(8,128)} %bitcast.3) | data formatting | bytes 2097152 | tf_op jit(solution)/shard_map/transpose | solution.py:327
  116.7 0.0 copy-done.1
  116.7 0.0 copy-start
  116.7 1.1 bitcast_subtract_fusion
  117.8 0.7 copy-done
  118.5 1.1 copy.10
  (1 shorter events, 0.0 us)
Async XLA Ops:
  2.3 114.4 %copy-start.1 = (f32[2,512,256]{2,1,0:T(8,128)S(1)}, f32[2,512,256]{2,1,0:T(8,128)}, u32[]{:S(2)}) copy-start(f32[2,512,256]{2,1,0:T(8,128)} %param.9) | copy-start | bytes 3145732
  116.7 1.8 %copy-start = (bf16[2,6,256,256]{3,2,1,0:T(8,128)(2,1)S(1)}, bf16[2,6,256,256]{3,2,1,0:T(8,128)(2,1)}, u32[]{:S(2)}) copy-start(bf16[2,6,256,256]{3,2,1,0:T(8,128)(2,1)} %get-tuple-element.8) | copy-start | bytes 4718596

commit v2 on v1

v2 whole, which is shorter than its diff:
```python
import functools

import jax
import jax.numpy as jnp
from jax import lax
from jax.experimental import pallas as pl
from jax.experimental.pallas import tpu as pltpu
from jax.sharding import PartitionSpec as P

MESH = pl.DeviceIdType.MESH
CHUNKS = 8
RING = 4
CAP = 6
LAG2, LAGM, LAG, AHEAD = 1, 1, 1, 2
ORDER = "12ecbm"


def dot(a, b):
    return jnp.dot(a, b, preferred_element_type=jnp.float32)


def dot_t(a, b):
    return lax.dot_general(a, b, (((1,), (1,)), ((), ())), preferred_element_type=jnp.float32)


def kernel(
    dest, target, panels, inverses, factor, summed,
    keys, table, pan, inv, minus, upd, mer, t1, g1, g2,
    psend, precv, isend, irecv, rsend, rrecv, load,
):
    n_chunks, _, leaves, rows_b, h, width = pan.shape
    part = inverses.shape[2]
    px, pc = lax.axis_index("prow"), lax.axis_index("pcol")
    x, core = px // 2, px % 2
    z, y = pc // RING, pc % RING

    def at_x(step, other=0):
        return ((x + step) % RING) * 2 + (core if not other else 1 - core)

    def at_yz(dy, dz):
        return ((z + dz) % RING) * RING + (y + dy) % RING

    x_next, x_prev, mate = (at_x(1), pc), (at_x(3), pc), (at_x(0, 1), pc)
    y_next, y_prev = (px, at_yz(1, 0)), (px, at_yz(3, 0))
    z_next, z_prev = (px, at_yz(0, 1)), (px, at_yz(0, 3))
    y_far, z_far = (px, at_yz(2, 0)), (px, at_yz(0, 2))

    def remote(src, dst, send, recv, device):
        return pltpu.make_async_remote_copy(
            src_ref=src, dst_ref=dst, send_sem=send, recv_sem=recv,
            device_id=device, device_id_type=MESH,
        )

    def gather_copy(view, send, recv, n):
        blocks = (px, px, px, at_x(3), at_x(1), at_x(3), at_x(1), at_x(2), at_x(2))
        planes = (None, None, None, 0, 1, None, None, 0, 1)
        devices = (x_next, x_prev, mate, x_next, x_prev, mate, mate, mate, mate)
        src = view(blocks[n], planes[n])
        return remote(src, src, send(n), recv(n), devices[n])

    def gather_wait(view, send, recv, n):
        blocks = (
            at_x(3), at_x(1), at_x(0, 1), at_x(2), at_x(2),
            at_x(3, 1), at_x(1, 1), at_x(2, 1), at_x(2, 1),
        )
        planes = (None, None, None, 0, 1, None, None, 0, 1)
        dst = view(blocks[n], planes[n])
        remote(dst, dst, send(n), recv(n), mate).wait_recv()

    def pan_args(k):
        def view(block, plane):
            return pan.at[k, :, :, block] if plane is None else pan.at[k, plane, :, block]

        return view, (lambda n: psend.at[k, n]), (lambda n: precv.at[k, n])

    def inv_view(block, plane):
        rows = pl.ds(pl.multiple_of(block * part, part), part)
        return inv.at[:, :, rows] if plane is None else inv.at[plane, :, rows]

    inv_args = (inv_view, (lambda n: isend.at[n]), (lambda n: irecv.at[n]))

    def sum_copy(k, half, n):
        along_y, along_z = (y_next, y_prev, y_far), (z_next, z_prev, z_far)
        first, then = (along_y, along_z) if half == 0 else (along_z, along_y)
        m, t, g, gg = mer.at[k, half], t1.at[k, half], g1.at[k, half], g2.at[k, half]
        src, dst, device = (
            (m.at[2, 0:2], t.at[0], first[0]),
            (m.at[2, 2:4], t.at[1], first[1]),
            (m.at[1, 2:4], g.at[0, 2:4], first[0]),
            (m.at[3, 0:2], g.at[1, 0:2], first[1]),
            (m.at[1, 0:2], g.at[0, 0:2], first[0]),
            (m.at[3, 2:4], g.at[1, 2:4], first[1]),
            (m.at[0, 2], gg.at[2], then[2]),
            (m.at[0, 1], gg.at[0], then[0]),
            (m.at[0, 3], gg.at[1], then[1]),
        )[n]
        return remote(src, dst, rsend.at[k, half * 9 + n], rrecv.at[k, half * 9 + n], device)

    def load_pan(k):
        rows = pl.ds(pl.multiple_of(k * h, h), h)
        return pltpu.make_async_copy(panels.at[:, :, rows], pan.at[k, :, :, px], load.at[k])

    def make_table():
        blocks = leaves * rows_b
        for s in range(leaves):
            for b in range(rows_b):
                keys[s * rows_b + b] = dest[s, 0, b] * 2 + target[s, 0, b]

        def slot(q, carry):
            entries = [jnp.int32(blocks)] * CAP
            for block in range(blocks):
                match = keys[block] == q
                moved = [jnp.int32(block)] + entries[:-1]
                entries = [jnp.where(match, new, old) for new, old in zip(moved, entries)]
            for i in range(CAP):
                table[q * CAP + i] = entries[i]
            return carry

        lax.fori_loop(0, 2 * RING * RING, slot, 0)

    load_inv = pltpu.make_async_copy(inverses, inv_view(px, None), load.at[n_chunks])
    load_inv.start()
    for k in range(n_chunks):
        load_pan(k).start()

    barrier = pltpu.get_barrier_semaphore()
    neighbours = (x_next, x_prev, mate, y_next, y_prev, y_far, z_next, z_prev, z_far)
    for device in neighbours:
        pl.semaphore_signal(barrier, inc=1, device_id=device, device_id_type=MESH)
    upd[upd.shape[0] - 1] = jnp.zeros(upd.shape[1:], upd.dtype)
    pl.semaphore_wait(barrier, len(neighbours))

    load_inv.wait()
    for n in (0, 1, 2):
        gather_copy(*inv_args, n).start()
    for k in range(n_chunks):
        load_pan(k).wait()
    for n in (0, 1, 2):
        gather_copy(*pan_args(0), n).start()
    make_table()
    for n in (0, 1):
        gather_wait(*inv_args, n)
    for n in (3, 4, 5, 6):
        gather_copy(*inv_args, n).start()

    def in_turn(k, first, stage):
        @pl.when(jnp.logical_and(k >= first, k < n_chunks))
        def _():
            stage(k)

    def relay_first(k):
        for n in (0, 1):
            gather_wait(*pan_args(k), n)
        for n in (3, 4, 5, 6):
            gather_copy(*pan_args(k), n).start()

        if isinstance(k, int):
            for later in range(k + 1, k + 1 + AHEAD):
                for n in (0, 1, 2):
                    gather_copy(*pan_args(later), n).start()
            return

        @pl.when(k + AHEAD < n_chunks)
        def _():
            for n in (0, 1, 2):
                gather_copy(*pan_args(k + AHEAD), n).start()

    def relay_second(k):
        for n in (3, 4):
            gather_wait(*pan_args(k), n)
        for n in (7, 8):
            gather_copy(*pan_args(k), n).start()

    def relay_inverses():
        for n in (3, 4):
            gather_wait(*inv_args, n)
        for n in (7, 8):
            gather_copy(*inv_args, n).start()

    def make_factor():
        for n in (2, 5, 6, 7, 8):
            gather_wait(*inv_args, n)

        def leaf(s, carry):
            real = pan[:, 0, s, px].reshape(width, width)
            imag = pan[:, 1, s, px].reshape(width, width)
            inv_real, inv_imag = inv[0, s], inv[1, s]
            factor[0, s] = (dot(real, inv_real) - dot(imag, inv_imag)).astype(factor.dtype)
            turned = dot(real, inv_imag) + dot(imag, inv_real)
            factor[1, s] = turned.astype(factor.dtype)
            minus[s] = (-turned).astype(minus.dtype)
            return carry

        lax.fori_loop(0, leaves, leaf, 0)

    def multiply(k):
        for n in (2, 5, 6, 7, 8):
            gather_wait(*pan_args(k), n)

        def leaf(s, carry):
            real = pan[k, 0, s].reshape(rows_b * h, width)
            imag = pan[k, 1, s].reshape(rows_b * h, width)
            first = pl.multiple_of(s * rows_b, rows_b)
            product = dot_t(real, factor[0, s]) + dot_t(imag, minus[s])
            upd[pl.ds(first, rows_b), 0] = product.astype(upd.dtype).reshape(rows_b, h, width)
            product = dot_t(real, factor[1, s]) + dot_t(imag, factor[0, s])
            upd[pl.ds(first, rows_b), 1] = product.astype(upd.dtype).reshape(rows_b, h, width)
            return carry

        lax.fori_loop(0, leaves, leaf, 0, unroll=leaves)

        def merge(q, carry):
            half, f, g = q // 16, (q // 4) % 4, q % 4
            owner = at_yz(f + half * (g - f), g + half * (f - g))
            entry = (owner * 2 + half) * CAP
            total = upd[table[entry]].astype(jnp.float32)
            for i in range(1, CAP):
                total += upd[table[entry + i]].astype(jnp.float32)
            mer[k, half, f, g] = total.astype(mer.dtype)
            return carry

        lax.fori_loop(0, 32, merge, 0, unroll=2)
        for n in (0, 1, 2, 3):
            for half in (0, 1):
                sum_copy(k, half, n).start()

    def add_to(ref, other):
        ref[...] = (ref[...].astype(jnp.float32) + other[...].astype(jnp.float32)).astype(ref.dtype)

    def sum_b(k):
        for half in (0, 1):
            for n in (0, 1):
                sum_copy(k, half, n).wait_recv()
            add_to(mer.at[k, half, 1, 0:2], t1.at[k, half, 0])
            add_to(mer.at[k, half, 3, 2:4], t1.at[k, half, 1])
        for half in (0, 1):
            for n in (4, 5):
                sum_copy(k, half, n).start()

    def sum_c(k):
        for half in (0, 1):
            for n in (2, 3, 4, 5):
                sum_copy(k, half, n).wait_recv()
            total = mer[k, half, 0].astype(jnp.float32)
            total += g1[k, half, 0].astype(jnp.float32)
            total += g1[k, half, 1].astype(jnp.float32)
            mer[k, half, 0] = total.astype(mer.dtype)
        for n in (6, 7, 8):
            for half in (0, 1):
                sum_copy(k, half, n).start()

    def sum_e(k):
        for half in (0, 1):
            for n in (6, 7, 8):
                sum_copy(k, half, n).wait_recv()
            total = mer[k, half, 0, 0].astype(jnp.float32)
            for n in range(3):
                total += g2[k, half, n].astype(jnp.float32)
            rows = pl.ds(pl.multiple_of(k * h, h), h)
            summed[half, :, rows] = total
        for n in range(9):
            gather_copy(*pan_args(k), n).wait_send()
            for half in (0, 1):
                sum_copy(k, half, n).wait_send()

    relay_first(0)
    relay_inverses()
    relay_second(0)
    make_factor()
    multiply(0)

    stages = {
        "1": (0, 1, relay_first), "2": (LAG2, 1, relay_second), "m": (LAGM, 1, multiply),
        "b": (LAGM + LAG, 0, sum_b), "c": (LAGM + 2 * LAG, 0, sum_c),
        "e": (LAGM + 3 * LAG, 0, sum_e),
    }

    def step(i, carry):
        for name in ORDER:
            lag, first, stage = stages[name]
            in_turn(i - lag, first, stage)
        return carry

    lax.fori_loop(1, n_chunks + LAGM + 3 * LAG, step, 0)

    for n in range(9):
        gather_copy(*inv_args, n).wait_send()


def finish(factor, summed, ancestors, factor_out, schur, res, out, fac_out):
    rows = summed.shape[2]
    keep = [
        pltpu.make_async_copy(factor.at[n], factor_out.at[n], fac_out.at[n]) for n in (0, 1)
    ]
    for one in keep:
        one.start()
    for t in (0, 1):
        for plane in (0, 1):
            here = pl.ds(t * rows, rows)
            res[plane, here] = ancestors[plane, here] - summed[t, plane].T
            store = pltpu.make_async_copy(
                res.at[plane, here], schur.at[plane, here], out.at[t, plane]
            )
            store.start()
            keep.append(store)
    for one in keep:
        one.wait()


def local(panels, inverses, dest, target, ancestors):
    panels = pltpu.with_memory_space_constraint(panels, pltpu.HBM)
    inverses = pltpu.with_memory_space_constraint(inverses, pltpu.HBM)
    _, leaves, rows, width = panels.shape
    rows_b = dest.shape[2]
    h = rows // CHUNKS
    blocks = leaves * rows_b
    bf16, f32 = jnp.bfloat16, jnp.float32
    any_space = pl.BlockSpec(memory_space=pl.ANY)
    vmem = pl.BlockSpec(memory_space=pltpu.VMEM)
    smem = pl.BlockSpec(memory_space=pltpu.SMEM)
    hbm = pl.BlockSpec(memory_space=pltpu.HBM)
    dma = pltpu.SemaphoreType.DMA
    factor, summed = pl.pallas_call(
        kernel,
        out_shape=(
            jax.ShapeDtypeStruct(panels.shape, bf16),
            jax.ShapeDtypeStruct((2, 2, rows, width), f32),
        ),
        in_specs=[smem, smem, hbm, hbm],
        out_specs=(vmem, vmem),
        scratch_shapes=[
            pltpu.SMEM((blocks,), jnp.int32),
            pltpu.SMEM((2 * RING * RING * CAP,), jnp.int32),
            pltpu.VMEM((CHUNKS, 2, leaves, rows_b, h, width), bf16),
            pltpu.VMEM((2, leaves, width, width), bf16),
            pltpu.VMEM((leaves, rows, width), bf16),
            pltpu.VMEM((blocks + 1, 2, h, width), bf16),
            pltpu.VMEM((CHUNKS, 2, 4, 4, 2, h, width), bf16),
            pltpu.VMEM((CHUNKS, 2, 2, 2, 2, h, width), bf16),
            pltpu.VMEM((CHUNKS, 2, 2, 4, 2, h, width), bf16),
            pltpu.VMEM((CHUNKS, 2, 3, 2, h, width), bf16),
            dma((CHUNKS, 9)), dma((CHUNKS, 9)), dma((9,)), dma((9,)),
            dma((CHUNKS, 18)), dma((CHUNKS, 18)), dma((CHUNKS + 1,)),
        ],
        compiler_params=pltpu.CompilerParams(
            collective_id=0, has_side_effects=True, vmem_limit_bytes=40 * 1024 * 1024
        ),
    )(dest, target, panels, inverses)
    return pl.pallas_call(
        finish,
        out_shape=(
            jax.ShapeDtypeStruct(panels.shape, bf16),
            jax.ShapeDtypeStruct(ancestors.shape, f32),
        ),
        in_specs=[vmem, vmem, vmem],
        out_specs=(any_space, any_space),
        scratch_shapes=[pltpu.VMEM(ancestors.shape, f32), dma((2, 2)), dma((2,))],
        compiler_params=pltpu.CompilerParams(vmem_limit_bytes=8 * 1024 * 1024),
    )(factor, summed, ancestors)


def solution(mesh):
    return jax.shard_map(
        local,
        mesh=mesh,
        in_specs=(
            P(None, "pcol", "prow", None),
            P(None, "pcol", "prow", None),
            P("pcol", "prow", None),
            P("pcol", "prow", None),
            P(None, "prow", "pcol"),
        ),
        out_specs=(P(None, "pcol", "prow", None), P(None, "prow", "pcol")),
        check_vma=False,
    )
```

time: 120 us -> 96.4 us (0.80)
  Pallas kernels: 113 us -> 94.1 us
  other arithmetic: 2.67 us -> 0 us
  local copies, waits for them, and re-layouts: 3.45 us -> 1.45 us
    pallas_call x1, Pallas kernels: 113 us -> 92.6 us  [local(): pl.pallas_call(kernel, out_shape=(jax.ShapeDtypeStruct(panels.shape, bf16...]
    transpose x1 -> x0, local copies, waits for them, and re-layouts: 1.56 us -> none  [local(): summed = summed.transpose(1, 0, 3, 2).reshape(ancestors.shape)]
    pallas_call x0 -> x1, Pallas kernels: none -> 1.53 us  [local(): pl.pallas_call(finish, out_shape=(jax.ShapeDtypeStruct(panels.shape, bf16...]
where the time goes in v2:
time: 96.4 us; the launch traced here: 96.2 us
  Pallas kernels  94.1 us (98%)
  local copies, waits for them, and re-layouts  1.45 us (2%)
    pallas_call x1, Pallas kernels, local(): pl.pallas_call(kernel, out_shape=(jax.ShapeDtypeStruct(panels.shape, bf16...  92.6 us

profile of v2, /device:TPU:0, one launch (start us, length us, event | category | flops | bytes accessed | tf_op | source)
XLA Modules:
  0.0 96.2 jit_solution(8723299083423974293)
XLA Ops:
  0.6 0.0 copy-start
  0.6 0.0 copy-start.1
  0.7 0.8 copy-done.1
  1.4 0.0 copy-start.2
  1.4 0.7 copy-done.2
  2.1 92.6 %shard_map.68 = (bf16[2,6,256,256]{3,2,1,0:T(8,128)(2,1)S(1)}, f32[2,2,256,256]{3,2,1,0:T(8,128)S(1)}) custom-call(s32[6,1,8]{2,1,0:T(1,128)S(1)} %copy-done.1, s32[6,1,8]{2,1,0:T(1,128)S(1)} %copy-done.2, bf16[2,6,256,256]{3,2,1,0:T(8,128)(2,1)} %panels.1, bf16[2,6,32,256]{3,2,1,0:T(8,128)(2,1)} %inverses.1), custom_call_target="tpu_custom_call" | custom-call | tf_op jit(solution)/shard_map/pallas_call | solution.py:323
  94.7 0.0 copy-done
  94.7 1.5 %shard_map.69 = (bf16[2,6,256,256]{3,2,1,0:T(8,128)(2,1)}, f32[2,512,256]{2,1,0:T(8,128)}) custom-call(bf16[2,6,256,256]{3,2,1,0:T(8,128)(2,1)S(1)} %get-tuple-element.4.factor, f32[2,2,256,256]{3,2,1,0:T(8,128)S(1)} %get-tuple-element.5.summed, f32[2,512,256]{2,1,0:T(8,128)S(1)} %copy-done), custom_call_target="tpu_custom_call" | custom-call | tf_op jit(solution)/shard_map/pallas_call | solution.py:349
Async XLA Ops:
  0.6 94.0 %copy-start = (f32[2,512,256]{2,1,0:T(8,128)S(1)}, f32[2,512,256]{2,1,0:T(8,128)}, u32[]{:S(2)}) copy-start(f32[2,512,256]{2,1,0:T(8,128)} %ancestors.1) | copy-start | bytes 3145732
  0.6 0.8 copy-start.1
  1.4 0.7 copy-start.2

commit v3 on v2

--- a/solution.py
+++ b/solution.py
@@ -11,8 +11,10 @@
 CHUNKS = 8
 RING = 4
 CAP = 6
-LAG2, LAGM, LAG, AHEAD = 1, 1, 1, 2
-ORDER = "12ecbm"
+AHEAD = 2
+LOOP = (("1", 0), ("e", 4), ("c", 3), ("2", 1), ("b", 2), ("m", 1))
+UNROLL = 4
+WAITED = (0, 0, 2, 1, 1, 2, 2, 2, 2)
 
 
 def dot(a, b):
@@ -25,7 +27,7 @@
 
 def kernel(
     dest, target, panels, inverses, factor, summed,
-    keys, table, pan, inv, minus, upd, mer, t1, g1, g2,
+    dests, targets, keys, table, pan, inv, minus, upd, mer, t1, g1, g2,
     psend, precv, isend, irecv, rsend, rrecv, load,
 ):
     n_chunks, _, leaves, rows_b, h, width = pan.shape
@@ -56,28 +58,31 @@
         planes = (None, None, None, 0, 1, None, None, 0, 1)
         devices = (x_next, x_prev, mate, x_next, x_prev, mate, mate, mate, mate)
         src = view(blocks[n], planes[n])
-        return remote(src, src, send(n), recv(n), devices[n])
-
-    def gather_wait(view, send, recv, n):
-        blocks = (
-            at_x(3), at_x(1), at_x(0, 1), at_x(2), at_x(2),
-            at_x(3, 1), at_x(1, 1), at_x(2, 1), at_x(2, 1),
-        )
-        planes = (None, None, None, 0, 1, None, None, 0, 1)
-        dst = view(blocks[n], planes[n])
-        remote(dst, dst, send(n), recv(n), mate).wait_recv()
+        return remote(src, src, send, recv.at[WAITED[n]], devices[n])
+
+    def gather_wait(view, send, recv, group):
+        part_of = view(0, None, (2, 1, 4)[group])
+        remote(part_of, part_of, send, recv.at[group], mate).wait_recv()
+
+    def gather_drain(view, send, recv):
+        part_of = view(0, None, 7)
+        remote(part_of, part_of, send, recv.at[0], mate).wait_send()
 
     def pan_args(k):
-        def view(block, plane):
+        def view(block, plane, count=None):
+            if count:
+                return pan.at[k, :, :, 0:count]
             return pan.at[k, :, :, block] if plane is None else pan.at[k, plane, :, block]
 
-        return view, (lambda n: psend.at[k, n]), (lambda n: precv.at[k, n])
-
-    def inv_view(block, plane):
+        return view, psend.at[k], precv.at[k]
+
+    def inv_view(block, plane, count=None):
+        if count:
+            return inv.at[:, :, 0 : count * part]
         rows = pl.ds(pl.multiple_of(block * part, part), part)
         return inv.at[:, :, rows] if plane is None else inv.at[plane, :, rows]
 
-    inv_args = (inv_view, (lambda n: isend.at[n]), (lambda n: irecv.at[n]))
+    inv_args = (inv_view, isend.at[0], irecv)
 
     def sum_copy(k, half, n):
         along_y, along_z = (y_next, y_prev, y_far), (z_next, z_prev, z_far)
@@ -94,17 +99,25 @@
             (m.at[0, 1], gg.at[0], then[0]),
             (m.at[0, 3], gg.at[1], then[1]),
         )[n]
-        return remote(src, dst, rsend.at[k, half * 9 + n], rrecv.at[k, half * 9 + n], device)
+        return remote(src, dst, rsend.at[k], rrecv.at[k, (0, 0, 1, 1, 1, 1, 2, 2, 2)[n]], device)
+
+    def sum_wait(k, group):
+        part_of = upd.at[0 : (8, 16, 6)[group]]
+        remote(part_of, part_of, rsend.at[k], rrecv.at[k, group], mate).wait_recv()
+
+    def sum_drain(k):
+        part_of = upd.at[0:30]
+        remote(part_of, part_of, rsend.at[k], rrecv.at[k, 0], mate).wait_send()
 
     def load_pan(k):
         rows = pl.ds(pl.multiple_of(k * h, h), h)
-        return pltpu.make_async_copy(panels.at[:, :, rows], pan.at[k, :, :, px], load.at[k])
+        return pltpu.make_async_copy(panels.at[:, :, rows], pan.at[k, :, :, px], load.at[0])
 
     def make_table():
         blocks = leaves * rows_b
         for s in range(leaves):
             for b in range(rows_b):
-                keys[s * rows_b + b] = dest[s, 0, b] * 2 + target[s, 0, b]
+                keys[s * rows_b + b] = dests[s, 0, b] * 2 + targets[s, 0, b]
 
         def slot(q, carry):
             entries = [jnp.int32(blocks)] * CAP
@@ -118,8 +131,12 @@
 
         lax.fori_loop(0, 2 * RING * RING, slot, 0)
 
-    load_inv = pltpu.make_async_copy(inverses, inv_view(px, None), load.at[n_chunks])
+    load_inv = pltpu.make_async_copy(inverses, inv_view(px, None), load.at[1])
+    load_dest = pltpu.make_async_copy(dest, dests, load.at[2])
+    load_target = pltpu.make_async_copy(target, targets, load.at[3])
     load_inv.start()
+    load_dest.start()
+    load_target.start()
     for k in range(n_chunks):
         load_pan(k).start()
 
@@ -133,13 +150,14 @@
     load_inv.wait()
     for n in (0, 1, 2):
         gather_copy(*inv_args, n).start()
-    for k in range(n_chunks):
-        load_pan(k).wait()
+    own = pan.at[:, :, :, px]
+    pltpu.make_async_copy(own, own, load.at[0]).wait()
     for n in (0, 1, 2):
         gather_copy(*pan_args(0), n).start()
+    load_dest.wait()
+    load_target.wait()
     make_table()
-    for n in (0, 1):
-        gather_wait(*inv_args, n)
+    gather_wait(*inv_args, 0)
     for n in (3, 4, 5, 6):
         gather_copy(*inv_args, n).start()
 
@@ -149,8 +167,7 @@
             stage(k)
 
     def relay_first(k):
-        for n in (0, 1):
-            gather_wait(*pan_args(k), n)
+        gather_wait(*pan_args(k), 0)
         for n in (3, 4, 5, 6):
             gather_copy(*pan_args(k), n).start()
 
@@ -166,20 +183,17 @@
                 gather_copy(*pan_args(k + AHEAD), n).start()
 
     def relay_second(k):
-        for n in (3, 4):
-            gather_wait(*pan_args(k), n)
+        gather_wait(*pan_args(k), 1)
         for n in (7, 8):
             gather_copy(*pan_args(k), n).start()
 
     def relay_inverses():
-        for n in (3, 4):
-            gather_wait(*inv_args, n)
+        gather_wait(*inv_args, 1)
         for n in (7, 8):
             gather_copy(*inv_args, n).start()
 
     def make_factor():
-        for n in (2, 5, 6, 7, 8):
-            gather_wait(*inv_args, n)
+        gather_wait(*inv_args, 2)
 
         def leaf(s, carry):
             real = pan[:, 0, s, px].reshape(width, width)
@@ -194,8 +208,7 @@
         lax.fori_loop(0, leaves, leaf, 0)
 
     def multiply(k):
-        for n in (2, 5, 6, 7, 8):
-            gather_wait(*pan_args(k), n)
+        gather_wait(*pan_args(k), 2)
 
         def leaf(s, carry):
             real = pan[k, 0, s].reshape(rows_b * h, width)
@@ -219,7 +232,7 @@
             mer[k, half, f, g] = total.astype(mer.dtype)
             return carry
 
-        lax.fori_loop(0, 32, merge, 0, unroll=2)
+        lax.fori_loop(0, 32, merge, 0, unroll=UNROLL)
         for n in (0, 1, 2, 3):
             for half in (0, 1):
                 sum_copy(k, half, n).start()
@@ -228,9 +241,8 @@
         ref[...] = (ref[...].astype(jnp.float32) + other[...].astype(jnp.float32)).astype(ref.dtype)
 
     def sum_b(k):
+        sum_wait(k, 0)
         for half in (0, 1):
-            for n in (0, 1):
-                sum_copy(k, half, n).wait_recv()
             add_to(mer.at[k, half, 1, 0:2], t1.at[k, half, 0])
             add_to(mer.at[k, half, 3, 2:4], t1.at[k, half, 1])
         for half in (0, 1):
@@ -238,9 +250,8 @@
                 sum_copy(k, half, n).start()
 
     def sum_c(k):
+        sum_wait(k, 1)
         for half in (0, 1):
-            for n in (2, 3, 4, 5):
-                sum_copy(k, half, n).wait_recv()
             total = mer[k, half, 0].astype(jnp.float32)
             total += g1[k, half, 0].astype(jnp.float32)
             total += g1[k, half, 1].astype(jnp.float32)
@@ -250,18 +261,15 @@
                 sum_copy(k, half, n).start()
 
     def sum_e(k):
+        sum_wait(k, 2)
         for half in (0, 1):
-            for n in (6, 7, 8):
-                sum_copy(k, half, n).wait_recv()
             total = mer[k, half, 0, 0].astype(jnp.float32)
             for n in range(3):
                 total += g2[k, half, n].astype(jnp.float32)
             rows = pl.ds(pl.multiple_of(k * h, h), h)
             summed[half, :, rows] = total
-        for n in range(9):
-            gather_copy(*pan_args(k), n).wait_send()
-            for half in (0, 1):
-                sum_copy(k, half, n).wait_send()
+        gather_drain(*pan_args(k))
+        sum_drain(k)
 
     relay_first(0)
     relay_inverses()
@@ -270,21 +278,18 @@
     multiply(0)
 
     stages = {
-        "1": (0, 1, relay_first), "2": (LAG2, 1, relay_second), "m": (LAGM, 1, multiply),
-        "b": (LAGM + LAG, 0, sum_b), "c": (LAGM + 2 * LAG, 0, sum_c),
-        "e": (LAGM + 3 * LAG, 0, sum_e),
+        "1": relay_first, "2": relay_second, "m": multiply, "b": sum_b, "c": sum_c, "e": sum_e
     }
 
     def step(i, carry):
-        for name in ORDER:
-            lag, first, stage = stages[name]
-            in_turn(i - lag, first, stage)
+        for name, lag in LOOP:
+            in_turn(i - lag, 1 if name in "12m" else 0, stages[name])
         return carry
 
-    lax.fori_loop(1, n_chunks + LAGM + 3 * LAG, step, 0)
-
-    for n in range(9):
-        gather_copy(*inv_args, n).wait_send()
+    last = max(lag for _, lag in LOOP)
+    lax.fori_loop(1, n_chunks + last, step, 0)
+
+    gather_drain(*inv_args)
 
 
 def finish(factor, summed, ancestors, factor_out, schur, res, out, fac_out):
@@ -310,6 +315,8 @@
 def local(panels, inverses, dest, target, ancestors):
     panels = pltpu.with_memory_space_constraint(panels, pltpu.HBM)
     inverses = pltpu.with_memory_space_constraint(inverses, pltpu.HBM)
+    dest = pltpu.with_memory_space_constraint(dest, pltpu.HBM)
+    target = pltpu.with_memory_space_constraint(target, pltpu.HBM)
     _, leaves, rows, width = panels.shape
     rows_b = dest.shape[2]
     h = rows // CHUNKS
@@ -317,7 +324,6 @@
     bf16, f32 = jnp.bfloat16, jnp.float32
     any_space = pl.BlockSpec(memory_space=pl.ANY)
     vmem = pl.BlockSpec(memory_space=pltpu.VMEM)
-    smem = pl.BlockSpec(memory_space=pltpu.SMEM)
     hbm = pl.BlockSpec(memory_space=pltpu.HBM)
     dma = pltpu.SemaphoreType.DMA
     factor, summed = pl.pallas_call(
@@ -326,9 +332,10 @@
             jax.ShapeDtypeStruct(panels.shape, bf16),
             jax.ShapeDtypeStruct((2, 2, rows, width), f32),
         ),
-        in_specs=[smem, smem, hbm, hbm],
+        in_specs=[hbm, hbm, hbm, hbm],
         out_specs=(vmem, vmem),
         scratch_shapes=[
+            pltpu.SMEM(dest.shape, jnp.int32), pltpu.SMEM(dest.shape, jnp.int32),
             pltpu.SMEM((blocks,), jnp.int32),
             pltpu.SMEM((2 * RING * RING * CAP,), jnp.int32),
             pltpu.VMEM((CHUNKS, 2, leaves, rows_b, h, width), bf16),
@@ -339,8 +346,8 @@
             pltpu.VMEM((CHUNKS, 2, 2, 2, 2, h, width), bf16),
             pltpu.VMEM((CHUNKS, 2, 2, 4, 2, h, width), bf16),
             pltpu.VMEM((CHUNKS, 2, 3, 2, h, width), bf16),
-            dma((CHUNKS, 9)), dma((CHUNKS, 9)), dma((9,)), dma((9,)),
-            dma((CHUNKS, 18)), dma((CHUNKS, 18)), dma((CHUNKS + 1,)),
+            dma((CHUNKS,)), dma((CHUNKS, 3)), dma((1,)), dma((3,)),
+            dma((CHUNKS,)), dma((CHUNKS, 3)), dma((4,)),
         ],
         compiler_params=pltpu.CompilerParams(
             collective_id=0, has_side_effects=True, vmem_limit_bytes=40 * 1024 * 1024

time: 96.4 us -> 89.9 us (0.933)
  Pallas kernels: 94.1 us -> 88.2 us
  local copies, waits for them, and re-layouts: 1.45 us -> 0.01 us
    pallas_call x1, Pallas kernels: 92.6 us -> 86.7 us  [local(): pl.pallas_call(kernel, out_shape=(jax.ShapeDtypeStruct(panels.shape, bf16...]
    unnamed x6 -> x2, local copies, waits for them, and re-layouts: 1.45 us -> 0.01 us
where the time goes in v3:
time: 89.9 us; the launch traced here: 88.9 us
  Pallas kernels  88.2 us (98%)
    pallas_call x1, Pallas kernels, local(): pl.pallas_call(kernel, out_shape=(jax.ShapeDtypeStruct(panels.shape, bf16...  86.7 us

profile of v3, /device:TPU:0, one launch (start us, length us, event | category | flops | bytes accessed | tf_op | source)
XLA Modules:
  0.0 88.9 jit_solution(18162110232777573725)
XLA Ops:
  0.6 0.0 copy-start
  0.6 86.7 %shard_map.68 = (bf16[2,6,256,256]{3,2,1,0:T(8,128)(2,1)S(1)}, f32[2,2,256,256]{3,2,1,0:T(8,128)S(1)}) custom-call(s32[6,1,8]{2,1,0:T(1,128)} %dest.1, s32[6,1,8]{2,1,0:T(1,128)} %target.1, bf16[2,6,256,256]{3,2,1,0:T(8,128)(2,1)} %panels.1, bf16[2,6,32,256]{3,2,1,0:T(8,128)(2,1)} %inverses.1), custom_call_target="tpu_custom_call" | custom-call | tf_op jit(solution)/shard_map/pallas_call | solution.py:329
  87.3 0.0 copy-done
  87.3 1.5 %shard_map.69 = (bf16[2,6,256,256]{3,2,1,0:T(8,128)(2,1)}, f32[2,512,256]{2,1,0:T(8,128)}) custom-call(bf16[2,6,256,256]{3,2,1,0:T(8,128)(2,1)S(1)} %get-tuple-element.4.factor, f32[2,2,256,256]{3,2,1,0:T(8,128)S(1)} %get-tuple-element.5.summed, f32[2,512,256]{2,1,0:T(8,128)S(1)} %copy-done), custom_call_target="tpu_custom_call" | custom-call | tf_op jit(solution)/shard_map/pallas_call | solution.py:356
Async XLA Ops:
  0.6 86.7 %copy-start = (f32[2,512,256]{2,1,0:T(8,128)S(1)}, f32[2,512,256]{2,1,0:T(8,128)}, u32[]{:S(2)}) copy-start(f32[2,512,256]{2,1,0:T(8,128)} %ancestors.1) | copy-start | bytes 3145732

commit v4 on v3

--- a/solution.py
+++ b/solution.py
@@ -222,20 +222,35 @@
 
         lax.fori_loop(0, leaves, leaf, 0, unroll=leaves)
 
-        def merge(q, carry):
-            half, f, g = q // 16, (q // 4) % 4, q % 4
+        def merge(half, f, g):
             owner = at_yz(f + half * (g - f), g + half * (f - g))
             entry = (owner * 2 + half) * CAP
             total = upd[table[entry]].astype(jnp.float32)
             for i in range(1, CAP):
                 total += upd[table[entry + i]].astype(jnp.float32)
             mer[k, half, f, g] = total.astype(mer.dtype)
-            return carry
-
-        lax.fori_loop(0, 32, merge, 0, unroll=UNROLL)
-        for n in (0, 1, 2, 3):
+
+        def farthest(q, carry):
+            merge(q // 4, 2, q % 4)
+            return carry
+
+        def beside(q, carry):
+            merge(q // 8, 1 + 2 * ((q // 4) % 2), q % 4)
+            return carry
+
+        def own(q, carry):
+            merge(q // 4, 0, q % 4)
+            return carry
+
+        lax.fori_loop(0, 8, farthest, 0, unroll=UNROLL)
+        for n in (0, 1):
             for half in (0, 1):
                 sum_copy(k, half, n).start()
+        lax.fori_loop(0, 16, beside, 0, unroll=UNROLL)
+        for n in (2, 3):
+            for half in (0, 1):
+                sum_copy(k, half, n).start()
+        lax.fori_loop(0, 8, own, 0, unroll=UNROLL)
 
     def add_to(ref, other):
         ref[...] = (ref[...].astype(jnp.float32) + other[...].astype(jnp.float32)).astype(ref.dtype)

time: 89.9 us -> 87.1 us (0.969)
  Pallas kernels: 88.2 us -> 86.1 us
    pallas_call x1, Pallas kernels: 86.7 us -> 84.6 us  [local(): pl.pallas_call(kernel, out_shape=(jax.ShapeDtypeStruct(panels.shape, bf16...]
where the time goes in v4:
time: 87.1 us; the launch traced here: 86.8 us
  Pallas kernels  86.1 us (99%)
    pallas_call x1, Pallas kernels, local(): pl.pallas_call(kernel, out_shape=(jax.ShapeDtypeStruct(panels.shape, bf16...  84.6 us

profile of v4, /device:TPU:0, one launch (start us, length us, event | category | flops | bytes accessed | tf_op | source)
XLA Modules:
  0.0 86.8 jit_solution(7766018655942983719)
XLA Ops:
  0.6 0.0 copy-start
  0.6 84.6 %shard_map.68 = (bf16[2,6,256,256]{3,2,1,0:T(8,128)(2,1)S(1)}, f32[2,2,256,256]{3,2,1,0:T(8,128)S(1)}) custom-call(s32[6,1,8]{2,1,0:T(1,128)} %dest.1, s32[6,1,8]{2,1,0:T(1,128)} %target.1, bf16[2,6,256,256]{3,2,1,0:T(8,128)(2,1)} %panels.1, bf16[2,6,32,256]{3,2,1,0:T(8,128)(2,1)} %inverses.1), custom_call_target="tpu_custom_call" | custom-call | tf_op jit(solution)/shard_map/pallas_call | solution.py:344
  85.2 0.0 copy-done
  85.2 1.5 %shard_map.69 = (bf16[2,6,256,256]{3,2,1,0:T(8,128)(2,1)}, f32[2,512,256]{2,1,0:T(8,128)}) custom-call(bf16[2,6,256,256]{3,2,1,0:T(8,128)(2,1)S(1)} %get-tuple-element.4.factor, f32[2,2,256,256]{3,2,1,0:T(8,128)S(1)} %get-tuple-element.5.summed, f32[2,512,256]{2,1,0:T(8,128)S(1)} %copy-done), custom_call_target="tpu_custom_call" | custom-call | tf_op jit(solution)/shard_map/pallas_call | solution.py:371
Async XLA Ops:
  0.6 84.6 %copy-start = (f32[2,512,256]{2,1,0:T(8,128)S(1)}, f32[2,512,256]{2,1,0:T(8,128)}, u32[]{:S(2)}) copy-start(f32[2,512,256]{2,1,0:T(8,128)} %ancestors.1) | copy-start | bytes 3145732

commit v5 on v4

--- a/solution.py
+++ b/solution.py
@@ -266,14 +266,15 @@
 
     def sum_c(k):
         sum_wait(k, 1)
-        for half in (0, 1):
-            total = mer[k, half, 0].astype(jnp.float32)
-            total += g1[k, half, 0].astype(jnp.float32)
-            total += g1[k, half, 1].astype(jnp.float32)
-            mer[k, half, 0] = total.astype(mer.dtype)
-        for n in (6, 7, 8):
+        for g, ready in ((2, None), (1, 6), (3, 7), (0, 8)):
             for half in (0, 1):
-                sum_copy(k, half, n).start()
+                total = mer[k, half, 0, g].astype(jnp.float32)
+                total += g1[k, half, 0, g].astype(jnp.float32)
+                total += g1[k, half, 1, g].astype(jnp.float32)
+                mer[k, half, 0, g] = total.astype(mer.dtype)
+            if ready:
+                for half in (0, 1):
+                    sum_copy(k, half, ready).start()
 
     def sum_e(k):
         sum_wait(k, 2)

time: 87.1 us -> 87.1 us (level)
  no operation moved by 1% of the time
where the time goes in v5:
time: 87.1 us; the launch traced here: 86.7 us
  Pallas kernels  86.1 us (99%)
    pallas_call x1, Pallas kernels, local(): pl.pallas_call(kernel, out_shape=(jax.ShapeDtypeStruct(panels.shape, bf16...  84.5 us

profile of v5, /device:TPU:0, one launch (start us, length us, event | category | flops | bytes accessed | tf_op | source)
XLA Modules:
  0.0 86.7 jit_solution(10566143435095404607)
XLA Ops:
  0.6 0.0 copy-start
  0.6 84.5 %shard_map.68 = (bf16[2,6,256,256]{3,2,1,0:T(8,128)(2,1)S(1)}, f32[2,2,256,256]{3,2,1,0:T(8,128)S(1)}) custom-call(s32[6,1,8]{2,1,0:T(1,128)} %dest.1, s32[6,1,8]{2,1,0:T(1,128)} %target.1, bf16[2,6,256,256]{3,2,1,0:T(8,128)(2,1)} %panels.1, bf16[2,6,32,256]{3,2,1,0:T(8,128)(2,1)} %inverses.1), custom_call_target="tpu_custom_call" | custom-call | tf_op jit(solution)/shard_map/pallas_call | solution.py:345
  85.2 0.0 copy-done
  85.2 1.5 %shard_map.69 = (bf16[2,6,256,256]{3,2,1,0:T(8,128)(2,1)}, f32[2,512,256]{2,1,0:T(8,128)}) custom-call(bf16[2,6,256,256]{3,2,1,0:T(8,128)(2,1)S(1)} %get-tuple-element.4.factor, f32[2,2,256,256]{3,2,1,0:T(8,128)S(1)} %get-tuple-element.5.summed, f32[2,512,256]{2,1,0:T(8,128)S(1)} %copy-done), custom_call_target="tpu_custom_call" | custom-call | tf_op jit(solution)/shard_map/pallas_call | solution.py:372
Async XLA Ops:
  0.6 84.6 %copy-start = (f32[2,512,256]{2,1,0:T(8,128)S(1)}, f32[2,512,256]{2,1,0:T(8,128)}, u32[]{:S(2)}) copy-start(f32[2,512,256]{2,1,0:T(8,128)} %ancestors.1) | copy-start | bytes 3145732
